TPU v7x, 32 devices: a whole 2x2x4 slice. The times are simulated.
32 devices in a mesh: gx: 8 (over y, x, core), gy: 4 (over z).
Axes of the slice: x: 2, y: 2, z: 4, core: 2. Of those that a mesh axis runs over, the one named last changes fastest.
Arguments:
- products: bfloat16 [1536, 3, 2048], P('gy', None, 'gx'), may hold values from -6 to 6
- operator: bfloat16 [1536, 1536], P(None, 'gy'), may hold values from -0.21875 to 0.21875
Outputs:
- derivative: bfloat16 [1536, 3, 2048], P(('gy', 'gx'))
All inputs are finite; a program needn't handle non-finite values.
Results may differ from a plain program's by a relative error of at most 0.002.
Values may be sent and summed in bfloat16 or wider, within the bound.
No kernel may reach another device: no remote copies, remote signals or barrier semaphores. Data moves between devices by JAX's collectives and lax.ppermute only.
A program may use at most 64 MiB of HBM per device.

v0:
```python
import jax
import jax.numpy as jnp
from jax import lax
from jax.sharding import PartitionSpec as P


def body(products, operator):
    y_local, three, m_local = products.shape
    flat = products.reshape(y_local, three * m_local)
    summed = lax.psum_scatter(
        jnp.dot(operator, flat, preferred_element_type=jnp.float32),
        "gy",
        scatter_dimension=0,
        tiled=True,
    )
    result = summed.astype(jnp.bfloat16).reshape(y_local, three, m_local)
    return lax.all_to_all(result, "gx", split_axis=0, concat_axis=2, tiled=True)


def solution(mesh):
    return jax.shard_map(
        body,
        mesh=mesh,
        in_specs=(P("gy", None, "gx"), P(None, "gy")),
        out_specs=P(("gy", "gx"), None, None),
        check_vma=False,
    )
```

profile of v0, /device:TPU:0, one launch (start us, length us, event | category | flops | bytes accessed | tf_op | source)
XLA Modules:
  0.0 125.9 jit_solution(14700882482431408080)
XLA Ops:
  6.5 0.0 copy-start
  6.5 0.0 reduce-scatter.2.cloned.1.call-start
  6.5 1.5 %copy.14 = bf16[384,3,256]{0,2,1:T(8,128)(2,1)S(1)} copy(bf16[384,3,256]{2,0,1:T(8,128)(2,1)} %param.2) | data formatting | bytes 1179648 | tf_op args[0]
  8.0 0.0 copy-done
  8.0 3.5 %fusion = f32[1536,768]{1,0:T(8,128)} fusion(bf16[1536,384]{1,0:T(8,128)(2,1)S(1)} %copy-done, bf16[384,768]{0,1:T(8,128)(2,1)S(1)} %bitcast.9), kind=kOutput, calls=%fused_computation | convolution fusion | flops 905969664 | bytes 6488064 | tf_op jit(solution)/shard_map/dot_general | solution.py:11
  11.5 0.0 reduce-scatter.2.cloned.1.call-update
  11.6 88.2 %reduce-scatter.2.cloned.1.call-done = f32[384,768]{1,0:T(8,128)} async-done(((f32[1536,768]{1,0:T(8,128)}), f32[384,768]{1,0:T(8,128)}) %reduce-scatter.2.cloned.1.call-update) | async-done | bytes 1179664 | tf_op jit(solution)/shard_map/reduce_scatter | solution.py:10
  99.7 1.3 %convert_element_type.3 = bf16[384,768]{1,0:T(8,128)(2,1)S(1)} convert(f32[384,768]{1,0:T(8,128)} %reduce-scatter.2.cloned.1.call-done) | non-fusion elementwise | flops 294912 | bytes 1769472 | tf_op jit(solution)/shard_map/convert_element_type | solution.py:16
  101.1 0.3 copy.15
  101.4 0.8 copy.16
  102.2 16.0 %all_to_all.18 = bf16[384,3,256]{2,1,0:T(4,128)(2,1)S(1)} all-to-all(bf16[384,3,256]{2,1,0:T(4,128)(2,1)S(1)} %copy.16), channel_id=1, replica_groups=mesh['gx'=8,'gy'=4] {'gx'}, dimensions={0} | all-to-all | bytes 1179648 | tf_op jit(solution)/shard_map/all_to_all | solution.py:17
  118.1 0.1 copy.17
  118.2 0.9 copy.19
Async XLA Ops:
  6.5 1.5 %copy-start = (bf16[1536,384]{1,0:T(8,128)(2,1)S(1)}, bf16[1536,384]{1,0:T(8,128)(2,1)}, u32[]{:S(2)}) copy-start(bf16[1536,384]{1,0:T(8,128)(2,1)} %param.3) | copy-start | bytes 3538948
  6.5 93.2 %reduce-scatter.2.cloned.1.call-start = ((), (), s32[]{:S(2)}) async-start(), calls=%async_computation.2 | async-start | bytes 5898240 | tf_op jit(solution)/shard_map/reduce_scatter | solution.py:10
Sparse Core Ops, SparseCore 0:
  11.7 88.0 reduce-scatter.1
where the time goes:
time: 126 us
  waiting for transfers between devices  88.2 us (70%)
  blocking collectives  16 us (13%)
  between operations  13.4 us (11%)
  matrix products  3.53 us (3%)
  local copies, waits for them, and re-layouts  3.49 us (3%)
  other arithmetic  1.33 us (1%)
    reduce_scatter x1, waiting for transfers between devices, body(): lax.psum_scatter(jnp.dot(operator, flat, preferred_element_type=jnp.float...  88.2 us
    all_to_all x1, blocking collectives, body(): return lax.all_to_all(result, 'gx', split_axis=0, concat_axis=2, tiled=True)  16 us
    dot_general x1, matrix products, body(): jnp.dot(operator, flat, preferred_element_type=jnp.float32)  3.53 us
  transfers between devices with their start and end apart: 1, of which 1 were waited for; matrix products, arithmetic and copies ran while one was open for 0% of the time, Pallas kernels for 0%

commit v1 on v0

--- a/solution.py
+++ b/solution.py
@@ -14,7 +14,10 @@
         tiled=True,
     )
     result = summed.astype(jnp.bfloat16).reshape(y_local, three, m_local)
-    return lax.all_to_all(result, "gx", split_axis=0, concat_axis=2, tiled=True)
+    return jnp.concatenate(
+        lax.all_to_all(jnp.stack(jnp.split(result, lax.axis_size("gx"), axis=0)), "gx", 0, 0),
+        axis=2,
+    )
 
 
 def solution(mesh):

time: 126 us -> 124 us (0.984)
  blocking collectives: 16 us -> 13.8 us
    all_to_all x1, blocking collectives: 16 us -> 13.8 us  [body(): lax.all_to_all(jnp.stack(jnp.split(result, lax.axis_size('gx'), axis=0)),...]
where the time goes in v1:
time: 124 us
  waiting for transfers between devices  88.2 us (71%)
  blocking collectives  13.8 us (11%)
  between operations  13.5 us (11%)
  matrix products  3.53 us (3%)
  local copies, waits for them, and re-layouts  3.14 us (3%)
  other arithmetic  1.33 us (1%)
    reduce_scatter x1, waiting for transfers between devices, body(): lax.psum_scatter(jnp.dot(operator, flat, preferred_element_type=jnp.float...  88.2 us
    all_to_all x1, blocking collectives, body(): lax.all_to_all(jnp.stack(jnp.split(result, lax.axis_size('gx'), axis=0)),...  13.8 us
    dot_general x1, matrix products, body(): jnp.dot(operator, flat, preferred_element_type=jnp.float32)  3.53 us
  transfers between devices with their start and end apart: 1, of which 1 were waited for; matrix products, arithmetic and copies ran while one was open for 0% of the time, Pallas kernels for 0%

profile of v1, /device:TPU:0, one launch (start us, length us, event | category | flops | bytes accessed | tf_op | source)
XLA Modules:
  0.0 123.5 jit_solution(17565427176177870618)
XLA Ops:
  6.5 0.0 copy-start
  6.5 0.0 reduce-scatter.2.cloned.1.call-start
  6.5 1.5 %copy.7 = bf16[384,3,256]{0,2,1:T(8,128)(2,1)S(1)} copy(bf16[384,3,256]{2,0,1:T(8,128)(2,1)} %param.2) | data formatting | bytes 1179648 | tf_op args[0]
  8.0 0.0 copy-done
  8.0 3.5 %fusion.1 = f32[1536,768]{1,0:T(8,128)} fusion(bf16[1536,384]{1,0:T(8,128)(2,1)S(1)} %copy-done, bf16[384,768]{0,1:T(8,128)(2,1)S(1)} %bitcast.6), kind=kOutput, calls=%fused_computation.9 | convolution fusion | flops 905969664 | bytes 6488064 | tf_op jit(solution)/shard_map/dot_general | solution.py:11
  11.5 0.0 reduce-scatter.2.cloned.1.call-update
  11.6 88.2 %reduce-scatter.2.cloned.1.call-done = f32[384,768]{1,0:T(8,128)} async-done(((f32[1536,768]{1,0:T(8,128)}), f32[384,768]{1,0:T(8,128)}) %reduce-scatter.2.cloned.1.call-update) | async-done | bytes 1179664 | tf_op jit(solution)/shard_map/reduce_scatter | solution.py:10
  99.7 1.3 %convert_element_type.3 = bf16[384,768]{1,0:T(8,128)(2,1)S(1)} convert(f32[384,768]{1,0:T(8,128)} %reduce-scatter.2.cloned.1.call-done) | non-fusion elementwise | flops 294912 | bytes 1769472 | tf_op jit(solution)/shard_map/convert_element_type | solution.py:16
  101.9 0.1 copy.8
  102.0 13.8 %all_to_all.5 = bf16[8,48,3,256]{3,1,2,0:T(8,128)(2,1)S(1)} all-to-all(bf16[8,48,3,256]{3,1,2,0:T(8,128)(2,1)S(1)} %copy.8), channel_id=1, replica_groups=mesh['gx'=8,'gy'=4] {'gx'}, dimensions={0} | all-to-all | bytes 1179648 | tf_op jit(solution)/shard_map/all_to_all | solution.py:18
  115.8 0.9 copy.10
  (17 shorter events, 0.7 us)
Async XLA Ops:
  6.5 1.5 %copy-start = (bf16[1536,384]{1,0:T(8,128)(2,1)S(1)}, bf16[1536,384]{1,0:T(8,128)(2,1)}, u32[]{:S(2)}) copy-start(bf16[1536,384]{1,0:T(8,128)(2,1)} %param.3) | copy-start | bytes 3538948
  6.5 93.2 %reduce-scatter.2.cloned.1.call-start = ((), (), s32[]{:S(2)}) async-start(), calls=%async_computation.2 | async-start | bytes 5898240 | tf_op jit(solution)/shard_map/reduce_scatter | solution.py:10
Sparse Core Ops, SparseCore 0:
  11.7 88.0 reduce-scatter.1
